TPU v7x, 32 devices: a whole 2x2x4 slice. The times are simulated.
32 devices in a mesh: grp: 2 (over x), row: 16 (over z, y, core).
Axes of the slice: x: 2, y: 2, z: 4, core: 2. Of those that a mesh axis runs over, the one named last changes fastest.
Arguments:
- sequence_features: bfloat16 [256, 128, 64], P('grp', 'row'), parts along dimension 0, may hold values from -6 to 6
- edge_features: bfloat16 [256, 128, 128], P(('grp', 'row')), parts along dimension 0, may hold values from -6 to 6
- residue_features: bfloat16 [256, 384], P(('grp', 'row')), parts along dimension 0, may hold values from -6 to 6
- polymer_labels: int32 [256], P('grp'), parts along dimension 0, may hold values from 0 to 7, never falling along the last dimension, each value on 1 to 64 neighbouring positions
- polymer_membership: int32 [16, 128], P('grp'), parts along dimension 0, may hold values from 0 to 1, as said below
- present_residue_flags: int32 [256], P('grp'), parts along dimension 0, may hold values 0 or 1
- sequence_scaling_vector: float32 [64], replicated, may hold values from 0.1 to 1.9
- first_embedding_matrix: bfloat16 [64, 32], replicated, may hold values from -0.75 to 0.75
- second_embedding_matrix: bfloat16 [64, 32], replicated, may hold values from -0.75 to 0.75
- contraction_matrix: bfloat16 [1024, 128], replicated, may hold values from -0.375 to 0.375
- contraction_offset: float32 [128], replicated, may hold values from -3 to 3
- feedforward_scaling_vector: float32 [128], replicated, may hold values from 0.1 to 1.9
- feedforward_switch_matrix: bfloat16 [128, 512], replicated, may hold values from -0.5 to 0.5
- widening_matrix: bfloat16 [128, 512], replicated, may hold values from -0.5 to 0.5
- narrowing_matrix: bfloat16 [512, 128], replicated, may hold values from -0.25 to 0.25
- logit_scaling_vector: float32 [128], replicated, may hold values from 0.1 to 1.9
- edge_logit_matrix: bfloat16 [128, 16], replicated, may hold values from -2 to 2
- residue_scaling_vector: float32 [384], replicated, may hold values from 0.1 to 1.9
- asking_matrix: bfloat16 [384, 384], replicated, as said below
- lookup_matrix: bfloat16 [384, 384], replicated, as said below
- content_matrix: bfloat16 [384, 384], replicated, may hold values from -0.3125 to 0.3125
- heads_sigmoid_matrix: bfloat16 [384, 384], replicated, may hold values from -0.3125 to 0.3125
- heads_merge_matrix: bfloat16 [384, 384], replicated, may hold values from -0.3125 to 0.3125
Outputs:
- pair_out: bfloat16 [256, 128, 128], P(('grp', 'row')), parts along dimension 0
- single_out: bfloat16 [256, 384], P(('grp', 'row')), parts along dimension 0
There are 2 independent parts, one for each index of `grp`. A program takes and returns all parts, laid end to end along the dimension named above; an argument that names none is the same for every part. Nothing has to cross between parts.
Inputs may be any that keep to these rules, and one draw needn't show every extreme that they name: `polymer_labels`: never falling along the tokens. `polymer_membership`: entry [c, s] is 1 where chain c takes part in MSA row s; every chain takes part in exactly 64 rows. `present_residue_flags`: 1 marks a real token. `asking_matrix`: a real matrix. `lookup_matrix`: a real matrix.
All inputs are finite; a program needn't handle non-finite values.
Results may differ from a plain program's by a relative error of at most 0.012.
Values may be sent and summed in bfloat16 or wider, within the bound.
No kernel may reach another device: no remote copies, remote signals or barrier semaphores. Data moves between devices by JAX's collectives and lax.ppermute only.
A program may use at most 128 MiB of HBM per device.

v0:
```python
import math
import jax
import jax.numpy as jnp
from jax import lax
from jax.sharding import PartitionSpec as P

epsilon = 1e-05
highest = lax.Precision.HIGHEST


def standardize_features(values, scales):
    values = values.astype(jnp.float32)
    centred = values - jnp.mean(values, axis=-1, keepdims=True)
    spread = jnp.mean(centred * centred, axis=-1, keepdims=True)
    return centred * lax.rsqrt(spread + epsilon) * scales


def local(
    sequence_features,
    edge_features,
    residue_features,
    polymer_labels,
    polymer_membership,
    present_residue_flags,
    sequence_scaling_vector,
    first_embedding_matrix,
    second_embedding_matrix,
    contraction_matrix,
    contraction_offset,
    feedforward_scaling_vector,
    feedforward_switch_matrix,
    widening_matrix,
    narrowing_matrix,
    logit_scaling_vector,
    edge_logit_matrix,
    residue_scaling_vector,
    asking_matrix,
    lookup_matrix,
    content_matrix,
    heads_sigmoid_matrix,
    heads_merge_matrix,
):
    token_row_count = residue_features.shape[0]
    sequence_entries = sequence_features.shape[0]
    sequence_depth = sequence_features.shape[2]
    factor_channels_width = first_embedding_matrix.shape[1]
    pair_width = edge_features.shape[2]
    all_tokens = edge_features.shape[1]
    chains = polymer_membership.shape[0]
    heads = edge_logit_matrix.shape[1]
    single_width = residue_features.shape[1]
    head_size = single_width // heads
    first_token = lax.axis_index("row") * token_row_count
    onehot_all = (polymer_labels[:, None] == jnp.arange(chains, dtype=jnp.int32)[None, :]).astype(
        jnp.float32
    )
    onehot_mine = lax.dynamic_slice_in_dim(onehot_all, first_token, token_row_count, 0)
    pair_rows = polymer_membership.astype(jnp.float32)
    sequence_present_flags = jnp.dot(onehot_mine, pair_rows, precision=highest).T
    shared = jnp.dot(pair_rows, pair_rows.T, precision=highest)
    counts = jnp.dot(
        jnp.dot(onehot_mine, shared, precision=highest), onehot_all.T, precision=highest
    )
    standardized_sequences = standardize_features(
        sequence_features, sequence_scaling_vector
    ).astype(jnp.bfloat16)
    flattened_alignment = standardized_sequences.reshape(
        sequence_entries * token_row_count, sequence_depth
    )
    first_embedding_entries = (
        jnp.dot(
            flattened_alignment, first_embedding_matrix, preferred_element_type=jnp.float32
        ).reshape(sequence_entries, token_row_count, factor_channels_width)
        * sequence_present_flags[:, :, None]
    ).astype(jnp.bfloat16)
    left_flattened = first_embedding_entries.reshape(
        sequence_entries, token_row_count * factor_channels_width
    )
    second_embedding_entries = (
        jnp.dot(
            flattened_alignment, second_embedding_matrix, preferred_element_type=jnp.float32
        ).reshape(sequence_entries, token_row_count, factor_channels_width)
        * sequence_present_flags[:, :, None]
    ).astype(jnp.bfloat16)

    def finish_block(outer, column_start, stride_columns):
        shared_cols = lax.dynamic_slice_in_dim(counts, column_start, stride_columns, 1)
        outer = (outer / jnp.maximum(shared_cols, 1.0)[:, :, None]).astype(jnp.bfloat16)
        update = (
            jnp.dot(
                outer.reshape(
                    token_row_count * stride_columns, factor_channels_width * factor_channels_width
                ),
                contraction_matrix,
                preferred_element_type=jnp.float32,
            )
            + contraction_offset
        )
        old_cols = lax.dynamic_slice_in_dim(edge_features, column_start, stride_columns, 1).reshape(
            token_row_count * stride_columns, pair_width
        )
        return (
            (old_cols.astype(jnp.float32) + update)
            .astype(jnp.bfloat16)
            .reshape(token_row_count, stride_columns, pair_width)
        )

    factor_piece = lax.all_gather(second_embedding_entries, "row", axis=1, tiled=True)
    width = factor_piece.shape[1]
    stride_columns = math.gcd(width, 128)

    def one_block(offset):
        panel = lax.dynamic_slice_in_dim(factor_piece, offset, stride_columns, 1).reshape(
            sequence_entries, stride_columns * factor_channels_width
        )
        outer = lax.dot_general(
            left_flattened, panel, (((0,), (0,)), ((), ())), preferred_element_type=jnp.float32
        )
        outer = outer.reshape(
            token_row_count, factor_channels_width, stride_columns, factor_channels_width
        ).transpose(0, 2, 1, 3)
        outer = outer.reshape(
            token_row_count, stride_columns, factor_channels_width * factor_channels_width
        )
        return finish_block(outer, offset, stride_columns)

    blocks = lax.map(one_block, jnp.arange(0, width, stride_columns, dtype=jnp.int32))
    pair_one = blocks.transpose(1, 0, 2, 3).reshape(token_row_count, width, pair_width)
    flat_pair = pair_one.reshape(token_row_count * all_tokens, pair_width)
    normed_pair = standardize_features(flat_pair, feedforward_scaling_vector).astype(jnp.bfloat16)
    gated = jnp.dot(normed_pair, feedforward_switch_matrix, preferred_element_type=jnp.float32)
    lifted = jnp.dot(normed_pair, widening_matrix, preferred_element_type=jnp.float32)
    hidden = (jax.nn.silu(gated) * lifted).astype(jnp.bfloat16)
    pair_two = (
        flat_pair.astype(jnp.float32)
        + jnp.dot(hidden, narrowing_matrix, preferred_element_type=jnp.float32)
    ).astype(jnp.bfloat16)
    bias_normed = standardize_features(pair_two, logit_scaling_vector).astype(jnp.bfloat16)
    bias_rows = jnp.dot(bias_normed, edge_logit_matrix, preferred_element_type=jnp.float32)
    bias_heads = bias_rows.reshape(token_row_count, all_tokens, heads).transpose(2, 0, 1)
    pair_out = pair_two.reshape(token_row_count, all_tokens, pair_width)
    normed_single = standardize_features(residue_features, residue_scaling_vector).astype(
        jnp.bfloat16
    )
    query = jnp.dot(normed_single, asking_matrix, preferred_element_type=jnp.float32).astype(
        jnp.bfloat16
    )
    query_heads = query.reshape(token_row_count, heads, head_size)
    sigmoid_gate = jax.nn.sigmoid(
        jnp.dot(normed_single, heads_sigmoid_matrix, preferred_element_type=jnp.float32)
    )
    scale = 1.0 / math.sqrt(head_size)
    piece = lax.all_gather(normed_single, "row", axis=0, tiled=True)
    keys_piece = jnp.dot(piece, lookup_matrix, preferred_element_type=jnp.float32).astype(
        jnp.bfloat16
    )
    values_piece = jnp.dot(piece, content_matrix, preferred_element_type=jnp.float32).astype(
        jnp.bfloat16
    )
    width = keys_piece.shape[0]
    key_heads = keys_piece.reshape(width, heads, head_size)
    value_heads = values_piece.reshape(width, heads, head_size)
    scores = (
        jnp.einsum("ihd,jhd->hij", query_heads, key_heads, preferred_element_type=jnp.float32)
        * scale
    )
    scores = scores + bias_heads
    live = (present_residue_flags == 1)[None, None, :]
    scores = jnp.where(live, scores, -1e30)
    peak_old = jnp.full((heads, token_row_count), -1e30, jnp.float32)
    peak_new = jnp.maximum(peak_old, jnp.max(scores, axis=-1))
    expos = jnp.where(live, jnp.exp(scores - peak_new[:, :, None]), 0.0)
    total_new = jnp.sum(expos, axis=-1)
    accum_new = jnp.einsum(
        "hij,jhd->hid", expos.astype(jnp.bfloat16), value_heads, preferred_element_type=jnp.float32
    )
    mixed = accum_new / total_new[:, :, None]
    mixed = mixed.transpose(1, 0, 2).reshape(token_row_count, single_width)
    attended = (mixed * sigmoid_gate).astype(jnp.bfloat16)
    single_out = (
        residue_features.astype(jnp.float32)
        + jnp.dot(attended, heads_merge_matrix, preferred_element_type=jnp.float32)
    ).astype(jnp.bfloat16)
    return (pair_out, single_out)


def solution(mesh):
    placed = (
        P("grp", "row", None),
        P(("grp", "row"), None, None),
        P(("grp", "row"), None),
        P("grp"),
        P("grp", None),
        P("grp"),
        P(),
        P(),
        P(),
        P(),
        P(),
        P(),
        P(),
        P(),
        P(),
        P(),
        P(),
        P(),
        P(),
        P(),
        P(),
        P(),
        P(),
    )
    return jax.shard_map(
        local,
        mesh=mesh,
        in_specs=placed,
        out_specs=(P(("grp", "row"), None, None), P(("grp", "row"), None)),
        check_vma=False,
    )
```

profile of v0, /device:TPU:0, one launch (start us, length us, event | category | flops | bytes accessed | tf_op | source)
XLA Modules:
  0.0 77.5 jit_solution(2994039761496273403)
XLA Ops:
  7.2 0.0 copy-start
  7.2 0.0 copy-start.1
  7.2 0.0 copy-start.5
  7.2 0.0 copy-start.8
  7.2 0.0 all-gather.2.cloned.1.call-start
  7.3 0.8 %iota_compare_fusion = pred[128,8]{1,0:T(8,128)(4,1)S(1)} fusion(s32[128]{0:T(128)} %param.26), kind=kLoop, calls=%fused_computation.68 | loop fusion | flops 1024 | bytes 1536 | tf_op jit(solution)/shard_map/eq | solution.py:54
  8.1 0.9 %convert_reduce_fusion.1 = f32[128,8]{0,1:T(8,128)S(1)} fusion(bf16[128,8,64]{0,2,1:T(8,128)(2,1)} %param.23), kind=kLoop, calls=%fused_computation.50 | loop fusion | flops 130048 | bytes 135168 | tf_op jit(solution)/shard_map/reduce_sum | solution.py:13
  9.1 1.0 %fusion.42 = f32[128,8]{0,1:T(8,128)S(1)} fusion(bf16[128,8,64]{0,2,1:T(8,128)(2,1)} %param.23, f32[128,8]{0,1:T(8,128)S(1)} %broadcast_multiply_fusion.2), kind=kLoop, calls=%fused_computation.54 | loop fusion | flops 261120 | bytes 139264 | tf_op jit(solution)/shard_map/reduce_sum | solution.py:14
  10.1 0.8 %convolution_bitcast_fusion.3 = f32[128,8]{0,1:T(8,128)S(1)} fusion(s32[8,128]{1,0:T(8,128)} %param.27, pred[128,8]{1,0:T(8,128)(4,1)S(1)} %iota_compare_fusion, s32[]{:T(128)S(6)} %select_n.14), kind=kOutput, calls=%fused_computation.34 | convolution fusion | flops 99328 | bytes 9220 | tf_op jit(solution)/shard_map/dot_general | solution.py:59
  10.9 1.8 %fusion.19 = bf16[128,8,32]{0,2,1:T(8,128)(2,1)} fusion(f32[128,8]{0,1:T(8,128)S(1)} %convolution_bitcast_fusion.3, bf16[128,8,64]{0,2,1:T(8,128)(2,1)} %param.23, f32[64]{0:T(128)} %param.29, f32[128,8]{0,1:T(8,128)S(1)} %add_rsqrt_fusion.2, f32[128,8]{0,1:T(8,128)S(1)} %broadcast_multiply_fusion.2, bf16[64,32]{0,1:T(8,128)(2,1)} %param.31), kind=kOutput, calls=%fused_computation.17 | convolution fusion | flops 4587520 | bytes 213248 | tf_op jit(solution)/shard_map/dot_general | solution.py:80
  12.6 0.0 all-gather.2.cloned.1.call-update
  12.7 0.8 %convert_reduce_fusion.2 = f32[8]{0:T(128)S(1)} fusion(bf16[8,384]{1,0:T(8,128)(2,1)} %param.25), kind=kLoop, calls=%fused_computation.76 | loop fusion | flops 6136 | bytes 6176 | tf_op jit(solution)/shard_map/reduce_sum | solution.py:13
  13.5 0.9 %fusion.71 = f32[8]{0:T(128)S(1)} fusion(bf16[8,384]{1,0:T(8,128)(2,1)} %param.25, f32[8]{0:T(128)S(1)} %broadcast_multiply_fusion.3), kind=kLoop, calls=%fused_computation.79 | loop fusion | flops 12280 | bytes 6208 | tf_op jit(solution)/shard_map/reduce_sum | solution.py:14
  14.4 0.8 %fusion.73 = bf16[8,384]{1,0:T(8,128)(2,1)S(1)} fusion(bf16[8,384]{1,0:T(8,128)(2,1)} %param.25, f32[384]{0:T(512)} %param.40, f32[8]{0:T(128)S(1)} %add_rsqrt_fusion.3, f32[8]{0:T(128)S(1)} %broadcast_multiply_fusion.3), kind=kLoop, calls=%fused_computation.81 | loop fusion | flops 15360 | bytes 13888 | tf_op jit(solution)/shard_map/convert_element_type | solution.py:142
  15.1 23.4 %all_gather.7 = bf16[128,384]{1,0:T(8,128)(2,1)S(1)} all-gather(bf16[8,384]{1,0:T(8,128)(2,1)S(1)} %fusion.73), channel_id=1, replica_groups=mesh['grp'=2,'row'=16] {'row'}, dimensions={0}, use_global_device_ids=true | all-gather | bytes 104448 | tf_op jit(solution)/shard_map/all_gather | solution.py:153
  38.5 0.0 copy-done
  38.5 0.2 convolution_convert_fusion.1
  38.7 0.1 copy.36
  38.8 1.2 %convolution_convert_fusion.2 = bf16[8,384]{1,0:T(8,128)(2,1)S(1)} fusion(bf16[384,384]{1,0:T(8,128)(2,1)} %param.41, bf16[8,384]{1,0:T(8,128)(2,1)} %param.25, f32[384]{0:T(512)} %param.40, f32[8]{0:T(128)S(1)} %add_rsqrt_fusion.3, f32[8]{0:T(128)S(1)} %broadcast_multiply_fusion.3), kind=kOutput, calls=%fused_computation.33 | convolution fusion | flops 2377728 | bytes 308800 | tf_op jit(solution)/shard_map/dot_general | solution.py:145
  40.0 0.1 reshape.122
  40.2 1.2 %convolution_convert_fusion = bf16[128,384]{1,0:T(8,128)(2,1)S(1)} fusion(bf16[128,384]{1,0:T(8,128)(2,1)S(1)} %all_gather.7, bf16[384,384]{1,0:T(8,128)(2,1)} %param.43), kind=kOutput, calls=%fused_computation.12 | convolution fusion | flops 37797888 | bytes 491520 | tf_op jit(solution)/shard_map/dot_general | solution.py:157
  41.3 0.1 copy.38
  41.5 0.1 fusion.78
  41.6 0.1 fusion.81
  41.7 0.2 fusion.30
  41.9 0.0 copy-done.14
  41.9 0.1 broadcast_compare_fusion
  42.0 11.4 %all-gather.2.cloned.1.call-done = bf16[128,128,32]{0,2,1:T(8,128)(2,1)} async-done(((bf16[128,8,32]{0,2,1:T(8,128)(2,1)}), bf16[128,128,32]{0,2,1:T(8,128)(2,1)}) %all-gather.2.cloned.1.call-update) | async-done | bytes 1048592 | tf_op jit(solution)/shard_map/all_gather | solution.py:108
  53.4 4.0 %convolution_bitcast_fusion = f32[8,128,32,32]{1,2,3,0:T(8,128)} fusion(bf16[128,32,128]{2,1,0:T(8,128)(2,1)} %bitcast.86, f32[128,8]{0,1:T(8,128)S(1)} %convolution_bitcast_fusion.3, bf16[128,8,64]{0,2,1:T(8,128)(2,1)S(1)} %copy-done.1, f32[64]{0:T(128)S(1)} %copy-done.8, f32[128,8]{0,1:T(8,128)S(1)} %add_rsqrt_fusion.2, ...), kind=kOutput, calls=%fused_computation.2 | convolution fusion | flops 273022976 | bytes 5390592 | tf_op jit(solution)/shard_map/while/body/eval_jaxpr/dot_general | solution.py:116
  57.5 4.7 %copy.35 = f32[8,128,32,32]{1,0,3,2:T(8,128)S(1)} copy(f32[8,128,32,32]{1,2,3,0:T(8,128)} %convolution_bitcast_fusion) | data formatting | bytes 8388608 | tf_op jit(solution)/shard_map/while/body/eval_jaxpr/transpose | solution.py:121
  62.2 0.0 copy-start.3
  62.2 0.0 copy-start.9
  62.2 1.3 %fusion.92 = (f32[1024]{0:T(1024)S(1)}, f32[1024,128]{1,0:T(8,128)S(1)}) fusion(f32[128]{0:T(128)S(1)} %copy-done.15, bf16[1024,128]{1,0:T(8,128)(2,1)S(1)} %copy-done.11, f32[128,8,8,128]{3,2,1,0:T(8,128)S(1)} %bitcast.85, f32[1024]{0:T(1024)S(1)} %fusion.30, bf16[1024,128]{1,0:T(8,128)(2,1)S(1)} %bitcast.92), kind=kOutput, calls=%fused_computation.106 | convolution fusion | flops 271318016 | bytes 5251584 | tf_op jit(solution)/shard_map/while/body/eval_jaxpr/dot_general | solution.py:90
  63.5 0.4 multiply_reduce_fusion
  63.9 0.5 fusion.41
  64.4 0.0 copy-start.13
  64.4 0.0 copy-start.16
  64.4 0.0 copy-start.4
  64.4 0.0 copy-start.7
  64.4 2.0 %convert_reduce_fusion = (f32[1024]{0:T(1024)S(1)}, bf16[1024,128]{1,0:T(8,128)(2,1)S(1)}) fusion(f32[1024,128]{1,0:T(8,128)S(1)} %get-tuple-element.19, bf16[512,128]{1,0:T(8,128)(2,1)} %param.37, f32[1024,512]{1,0:T(8,128)S(1)} %fusion.41, bf16[128,512]{1,0:T(8,128)(2,1)} %param.35, f32[128]{0:T(128)S(1)} %copy-done.9, f32[1024]{0:T(1024)S(1)} %add_rsqrt_fusion.1, ...), kind=kOutput, calls=%fused_computation.41 | convolution fusion | flops 272628736 | bytes 3158528 | tf_op jit(solution)/shard_map/dot_general | solution.py:136
  66.5 0.0 copy-start.2
  66.5 0.4 fusion.36
  66.9 0.9 %convolution_bitcast_fusion.2 = f32[2,8,8,128]{3,1,2,0:T(8,128)S(1)} fusion(bf16[128,16]{0,1:T(8,128)(2,1)S(1)} %copy-done.13, bf16[1024,128]{1,0:T(8,128)(2,1)S(1)} %get-tuple-element.21, f32[128]{0:T(128)S(1)} %copy-done.16, f32[1024]{0:T(1024)S(1)} %add_rsqrt_fusion, f32[1024]{0:T(1024)S(1)} %broadcast_multiply_fusion), kind=kOutput, calls=%fused_computation.21 | convolution fusion | flops 4849664 | bytes 340480 | tf_op jit(solution)/shard_map/dot_general | solution.py:139
  67.8 0.2 fusion.93
  68.1 0.2 fusion.59
  68.2 0.2 fusion.21
  68.5 0.1 reshape.126
  68.6 2.0 %fusion.29 = bf16[8,384]{1,0:T(8,128)(2,1)} fusion(bf16[384,384]{1,0:T(8,128)(2,1)} %param.45, f32[8,384]{1,0:T(8,128)S(1)} %reshape.126, bf16[384,384]{1,0:T(8,128)(2,1)} %param.44, bf16[8,384]{1,0:T(8,128)(2,1)S(1)} %copy-done.4, f32[384]{0:T(512)S(1)} %copy-done.7, f32[8]{0:T(128)S(1)} %add_rsqrt_fusion.3, f32[8]{0:T(128)S(1)} %broadcast_multiply_fusion.3), kind=kOutput, calls=%fused_computation.32 | convolution fusion | flops 4758528 | bytes 616000 | tf_op jit(solution)/shard_map/dot_general | solution.py:182
  (32 shorter events, 0.1 us)
Async XLA Ops:
  7.2 31.3 %copy-start = (bf16[384,384]{1,0:T(8,128)(2,1)S(1)}, bf16[384,384]{1,0:T(8,128)(2,1)}, u32[]{:S(2)}) copy-start(bf16[384,384]{1,0:T(8,128)(2,1)} %param.42) | copy-start | bytes 884740
  7.2 34.5 %copy-start.10 = (s32[128]{0:T(128)S(1)}, s32[128]{0:T(128)}, u32[]{:S(2)}) copy-start(s32[128]{0:T(128)} %param.26) | copy-start | bytes 1540
  7.2 46.2 %copy-start.1 = (bf16[128,8,64]{0,2,1:T(8,128)(2,1)S(1)}, bf16[128,8,64]{0,2,1:T(8,128)(2,1)}, u32[]{:S(2)}) copy-start(bf16[128,8,64]{0,2,1:T(8,128)(2,1)} %param.23) | copy-start | bytes 393220
  7.2 34.3 %copy-start.5 = (s32[8,128]{1,0:T(8,128)S(1)}, s32[8,128]{1,0:T(8,128)}, u32[]{:S(2)}) copy-start(s32[8,128]{1,0:T(8,128)} %param.27) | copy-start | bytes 12292
  7.2 46.2 %copy-start.8 = (f32[64]{0:T(128)S(1)}, f32[64]{0:T(128)}, u32[]{:S(2)}) copy-start(f32[64]{0:T(128)} %param.29) | copy-start | bytes 772
  7.2 34.7 %copy-start.14 = (s32[128]{0:T(128)S(1)}, s32[128]{0:T(128)}, u32[]{:S(2)}) copy-start(s32[128]{0:T(128)} %param.28) | copy-start | bytes 1540
  7.2 46.2 %copy-start.6 = (bf16[64,32]{0,1:T(8,128)(2,1)S(1)}, bf16[64,32]{0,1:T(8,128)(2,1)}, u32[]{:S(2)}) copy-start(bf16[64,32]{0,1:T(8,128)(2,1)} %param.30) | copy-start | bytes 12292
  7.2 46.2 %all-gather.2.cloned.1.call-start = ((), (), s32[]{:S(2)}) async-start(), calls=%async_computation | async-start | bytes 1114112 | tf_op jit(solution)/shard_map/all_gather | solution.py:108
  57.5 4.7 %copy-start.11 = (bf16[1024,128]{1,0:T(8,128)(2,1)S(1)}, bf16[1024,128]{1,0:T(8,128)(2,1)}, u32[]{:S(2)}) copy-start(bf16[1024,128]{1,0:T(8,128)(2,1)} %param.32) | copy-start | bytes 786436
  57.5 4.7 %copy-start.12 = (bf16[8,128,128]{2,1,0:T(8,128)(2,1)S(1)}, bf16[8,128,128]{2,1,0:T(8,128)(2,1)}, u32[]{:S(2)}) copy-start(bf16[8,128,128]{2,1,0:T(8,128)(2,1)} %param.24) | copy-start | bytes 786436
  57.5 4.7 %copy-start.15 = (f32[128]{0:T(128)S(1)}, f32[128]{0:T(128)}, u32[]{:S(2)}) copy-start(f32[128]{0:T(128)} %param.33) | copy-start | bytes 1540
  62.2 1.7 %copy-start.3 = (bf16[128,512]{1,0:T(8,128)(2,1)S(1)}, bf16[128,512]{1,0:T(8,128)(2,1)}, u32[]{:S(2)}) copy-start(bf16[128,512]{1,0:T(8,128)(2,1)} %param.36) | copy-start | bytes 393220
  62.2 1.7 %copy-start.9 = (f32[128]{0:T(128)S(1)}, f32[128]{0:T(128)}, u32[]{:S(2)}) copy-start(f32[128]{0:T(128)} %param.34) | copy-start | bytes 1540
  64.4 2.5 %copy-start.13 = (bf16[128,16]{0,1:T(8,128)(2,1)S(1)}, bf16[128,16]{0,1:T(8,128)(2,1)}, u32[]{:S(2)}) copy-start(bf16[128,16]{0,1:T(8,128)(2,1)} %param.39) | copy-start | bytes 12292
  64.4 2.5 %copy-start.16 = (f32[128]{0:T(128)S(1)}, f32[128]{0:T(128)}, u32[]{:S(2)}) copy-start(f32[128]{0:T(128)} %param.38) | copy-start | bytes 1540
  64.4 4.2 %copy-start.4 = (bf16[8,384]{1,0:T(8,128)(2,1)S(1)}, bf16[8,384]{1,0:T(8,128)(2,1)}, u32[]{:S(2)}) copy-start(bf16[8,384]{1,0:T(8,128)(2,1)} %param.25) | copy-start | bytes 18436
  64.4 4.2 %copy-start.7 = (f32[384]{0:T(512)S(1)}, f32[384]{0:T(512)}, u32[]{:S(2)}) copy-start(f32[384]{0:T(512)} %param.40) | copy-start | bytes 4612
  66.5 4.1 %copy-start.2 = (bf16[1024,128]{1,0:T(8,128)(2,1)}, bf16[1024,128]{1,0:T(8,128)(2,1)S(1)}, u32[]{:S(2)}) copy-start(bf16[1024,128]{1,0:T(8,128)(2,1)S(1)} %get-tuple-element.21) | copy-start | bytes 786436
Sparse Core Ops, SparseCore 0:
  12.8 40.5 all-gather.1
where the time goes:
time: 77.9 us; the launch traced here: 77.5 us
  blocking collectives  23.4 us (30%)
  matrix products  16.8 us (22%)
  between operations  14.4 us (18%)
  waiting for transfers between devices  11.4 us (15%)
  other arithmetic  6.2 us (8%)
  local copies, waits for them, and re-layouts  5.24 us (7%)
    all_gather x1, blocking collectives, local(): piece = lax.all_gather(normed_single, 'row', axis=0, tiled=True)  23.4 us
    all_gather x1, waiting for transfers between devices, local(): lax.all_gather(second_embedding_entries, 'row', axis=1, tiled=True)  11.4 us
    transpose x1, local copies, waits for them, and re-layouts, one_block(): outer = outer.reshape(token_row_count, factor_channels_width, stride_colu...  4.68 us
    dot_general x1, matrix products, one_block(): lax.dot_general(left_flattened, panel, (((0,), (0,)), ((), ())), preferre...  4.04 us
    reduce_sum x4, other arithmetic, standardize_features(): spread = jnp.mean(centred * centred, axis=-1, keepdims=True)  2.55 us
    dot_general x1, matrix products, local(): jnp.dot(hidden, narrowing_matrix, preferred_element_type=jnp.float32)  2.04 us
    dot_general x1, matrix products, local(): jnp.dot(attended, heads_merge_matrix, preferred_element_type=jnp.float32)  2 us
    dot_general x1, matrix products, local(): jnp.dot(flattened_alignment, second_embedding_matrix, preferred_element_t...  1.76 us
  transfers between devices with their start and end apart: 1, of which 1 were waited for; matrix products, arithmetic and copies ran while one was open for 8% of the time, Pallas kernels for 0%

commit v1 on v0

--- a/solution.py
+++ b/solution.py
@@ -105,7 +105,12 @@
             .reshape(token_row_count, stride_columns, pair_width)
         )
 
-    factor_piece = lax.all_gather(second_embedding_entries, "row", axis=1, tiled=True)
+    ring = [second_embedding_entries]
+    for hop in range(15):
+        ring.append(lax.ppermute(ring[-1], "row", [(dev, (dev + 1) % 16) for dev in range(16)]))
+    factor_piece = jnp.roll(
+        jnp.concatenate(ring[::-1], axis=1), (lax.axis_index("row") + 1) * ring[0].shape[1], axis=1
+    )
     width = factor_piece.shape[1]
     stride_columns = math.gcd(width, 128)
 

time: 77.9 us -> 132 us (1.69)
  waiting for transfers between devices: 11.4 us -> 84.7 us
  between operations: 14.4 us -> 1.16 us
  blocking collectives: 23.4 us -> 18.2 us
  matrix products: 16.8 us -> 14.9 us
    ppermute x0 -> x15, waiting for transfers between devices: none -> 84.7 us  [local(): lax.ppermute(ring[-1], 'row', [(dev, (dev + 1) % 16) for dev in range(16)])]
    all_gather x1 -> x0, waiting for transfers between devices: 11.4 us -> none  [local(): lax.all_gather(second_embedding_entries, 'row', axis=1, tiled=True)]
    all_gather x1, blocking collectives: 23.4 us -> 18.2 us  [local(): piece = lax.all_gather(normed_single, 'row', axis=0, tiled=True)]
  transfers between devices with their start and end apart: 1 -> 15, of which waited for: 1 -> 14; matrix products, arithmetic and copies ran while one was open for 8% -> 4% of each run, Pallas kernels for 0% -> 0%
where the time goes in v1:
time: 132 us
  waiting for transfers between devices  84.7 us (64%)
  blocking collectives  18.2 us (14%)
  matrix products  14.9 us (11%)
  local copies, waits for them, and re-layouts  6.24 us (5%)
  other arithmetic  6.07 us (5%)
    ppermute x15, waiting for transfers between devices, local(): lax.ppermute(ring[-1], 'row', [(dev, (dev + 1) % 16) for dev in range(16)])  84.7 us
    all_gather x1, blocking collectives, local(): piece = lax.all_gather(normed_single, 'row', axis=0, tiled=True)  18.2 us
    transpose x1, local copies, waits for them, and re-layouts, one_block(): outer = outer.reshape(token_row_count, factor_channels_width, stride_colu...  4.68 us
    dot_general x1, matrix products, one_block(): lax.dot_general(left_flattened, panel, (((0,), (0,)), ((), ())), preferre...  2.82 us
  transfers between devices with their start and end apart: 15, of which 14 were waited for; matrix products, arithmetic and copies ran while one was open for 4% of the time, Pallas kernels for 0%

profile of v1, /device:TPU:0, one launch (start us, length us, event | category | flops | bytes accessed | tf_op | source)
XLA Modules:
  0.0 132.1 jit_solution(6625230283193086518)
XLA Ops:
  0.7 0.8 iota_compare_fusion
  1.5 0.9 convert_reduce_fusion.1
  2.4 1.0 fusion.42
  3.4 0.8 convolution_bitcast_fusion.3
  4.2 1.1 fusion.19
  5.3 0.5 collective-permute-start
  5.9 6.9 %collective-permute-done = bf16[128,8,32]{0,2,1:T(8,128)(2,1)S(1)} collective-permute-done((bf16[128,8,32]{0,2,1:T(8,128)(2,1)S(1)}, bf16[128,8,32]{0,2,1:T(8,128)(2,1)S(1)}, u32[]{:S(2)}, u32[]{:S(2)}) %collective-permute-start) | collective-permute-done | bytes 65568 | tf_op jit(solution)/shard_map/ppermute | solution.py:110
  12.8 6.4 %collective-permute-done.1 = bf16[128,8,32]{0,2,1:T(8,128)(2,1)S(1)} collective-permute-done((bf16[128,8,32]{0,2,1:T(8,128)(2,1)S(1)}, bf16[128,8,32]{0,2,1:T(8,128)(2,1)S(1)}, u32[]{:S(2)}, u32[]{:S(2)}) %collective-permute-start.1) | collective-permute-done | bytes 65568 | tf_op jit(solution)/shard_map/ppermute | solution.py:110
  19.2 6.4 %collective-permute-done.2 = bf16[128,8,32]{0,2,1:T(8,128)(2,1)S(1)} collective-permute-done((bf16[128,8,32]{0,2,1:T(8,128)(2,1)S(1)}, bf16[128,8,32]{0,2,1:T(8,128)(2,1)S(1)}, u32[]{:S(2)}, u32[]{:S(2)}) %collective-permute-start.2) | collective-permute-done | bytes 65568 | tf_op jit(solution)/shard_map/ppermute | solution.py:110
  25.6 0.8 convert_reduce_fusion.2
  26.4 5.6 %collective-permute-done.3 = bf16[128,8,32]{0,2,1:T(8,128)(2,1)S(1)} collective-permute-done((bf16[128,8,32]{0,2,1:T(8,128)(2,1)S(1)}, bf16[128,8,32]{0,2,1:T(8,128)(2,1)S(1)}, u32[]{:S(2)}, u32[]{:S(2)}) %collective-permute-start.3) | collective-permute-done | bytes 65568 | tf_op jit(solution)/shard_map/ppermute | solution.py:110
  32.0 6.4 %collective-permute-done.4 = bf16[128,8,32]{0,2,1:T(8,128)(2,1)S(1)} collective-permute-done((bf16[128,8,32]{0,2,1:T(8,128)(2,1)S(1)}, bf16[128,8,32]{0,2,1:T(8,128)(2,1)S(1)}, u32[]{:S(2)}, u32[]{:S(2)}) %collective-permute-start.4) | collective-permute-done | bytes 65568 | tf_op jit(solution)/shard_map/ppermute | solution.py:110
  38.4 0.9 fusion.71
  39.2 5.5 %collective-permute-done.5 = bf16[128,8,32]{0,2,1:T(8,128)(2,1)S(1)} collective-permute-done((bf16[128,8,32]{0,2,1:T(8,128)(2,1)S(1)}, bf16[128,8,32]{0,2,1:T(8,128)(2,1)S(1)}, u32[]{:S(2)}, u32[]{:S(2)}) %collective-permute-start.5) | collective-permute-done | bytes 65568 | tf_op jit(solution)/shard_map/ppermute | solution.py:110
  44.8 6.4 %collective-permute-done.6 = bf16[128,8,32]{0,2,1:T(8,128)(2,1)S(1)} collective-permute-done((bf16[128,8,32]{0,2,1:T(8,128)(2,1)S(1)}, bf16[128,8,32]{0,2,1:T(8,128)(2,1)S(1)}, u32[]{:S(2)}, u32[]{:S(2)}) %collective-permute-start.6) | collective-permute-done | bytes 65568 | tf_op jit(solution)/shard_map/ppermute | solution.py:110
  51.1 0.8 fusion.73
  51.9 18.2 %all_gather.3 = bf16[128,384]{1,0:T(8,128)(2,1)S(1)} all-gather(bf16[8,384]{1,0:T(8,128)(2,1)S(1)} %fusion.73), channel_id=1, replica_groups=mesh['grp'=2,'row'=16] {'row'}, dimensions={0}, use_global_device_ids=true | all-gather | bytes 104448 | tf_op jit(solution)/shard_map/all_gather | solution.py:158
  70.2 0.2 collective-permute-start.8
  70.3 0.2 convolution_convert_fusion.1
  70.5 6.0 %collective-permute-done.8 = bf16[128,8,32]{0,2,1:T(8,128)(2,1)S(1)} collective-permute-done((bf16[128,8,32]{0,2,1:T(8,128)(2,1)S(1)}, bf16[128,8,32]{0,2,1:T(8,128)(2,1)S(1)}, u32[]{:S(2)}, u32[]{:S(2)}) %collective-permute-start.8) | collective-permute-done | bytes 65568 | tf_op jit(solution)/shard_map/ppermute | solution.py:110
  76.6 1.2 convolution_convert_fusion
  77.7 5.2 %collective-permute-done.9 = bf16[128,8,32]{0,2,1:T(8,128)(2,1)S(1)} collective-permute-done((bf16[128,8,32]{0,2,1:T(8,128)(2,1)S(1)}, bf16[128,8,32]{0,2,1:T(8,128)(2,1)S(1)}, u32[]{:S(2)}, u32[]{:S(2)}) %collective-permute-start.9) | collective-permute-done | bytes 65568 | tf_op jit(solution)/shard_map/ppermute | solution.py:110
  82.9 1.2 convolution_convert_fusion.2
  84.1 5.2 %collective-permute-done.10 = bf16[128,8,32]{0,2,1:T(8,128)(2,1)S(1)} collective-permute-done((bf16[128,8,32]{0,2,1:T(8,128)(2,1)S(1)}, bf16[128,8,32]{0,2,1:T(8,128)(2,1)S(1)}, u32[]{:S(2)}, u32[]{:S(2)}) %collective-permute-start.10) | collective-permute-done | bytes 65568 | tf_op jit(solution)/shard_map/ppermute | solution.py:110
  89.3 0.1 fusion.78
  89.5 6.3 %collective-permute-done.11 = bf16[128,8,32]{0,2,1:T(8,128)(2,1)S(1)} collective-permute-done((bf16[128,8,32]{0,2,1:T(8,128)(2,1)S(1)}, bf16[128,8,32]{0,2,1:T(8,128)(2,1)S(1)}, u32[]{:S(2)}, u32[]{:S(2)}) %collective-permute-start.11) | collective-permute-done | bytes 65568 | tf_op jit(solution)/shard_map/ppermute | solution.py:110
  95.7 0.1 fusion.81
  95.8 6.3 %collective-permute-done.12 = bf16[128,8,32]{0,2,1:T(8,128)(2,1)S(1)} collective-permute-done((bf16[128,8,32]{0,2,1:T(8,128)(2,1)S(1)}, bf16[128,8,32]{0,2,1:T(8,128)(2,1)S(1)}, u32[]{:S(2)}, u32[]{:S(2)}) %collective-permute-start.12) | collective-permute-done | bytes 65568 | tf_op jit(solution)/shard_map/ppermute | solution.py:110
  102.1 0.1 copy.30
  102.3 0.1 reshape.122
  102.4 0.1 copy.32
  102.5 6.0 %collective-permute-done.13 = bf16[128,8,32]{0,2,1:T(8,128)(2,1)S(1)} collective-permute-done((bf16[128,8,32]{0,2,1:T(8,128)(2,1)S(1)}, bf16[128,8,32]{0,2,1:T(8,128)(2,1)S(1)}, u32[]{:S(2)}, u32[]{:S(2)}) %collective-permute-start.13) | collective-permute-done | bytes 65568 | tf_op jit(solution)/shard_map/ppermute | solution.py:110
  108.5 0.2 fusion.30
  108.7 6.2 %collective-permute-done.14 = bf16[128,8,32]{0,2,1:T(8,128)(2,1)S(1)} collective-permute-done((bf16[128,8,32]{0,2,1:T(8,128)(2,1)S(1)}, bf16[128,8,32]{0,2,1:T(8,128)(2,1)S(1)}, u32[]{:S(2)}, u32[]{:S(2)}) %collective-permute-start.14) | collective-permute-done | bytes 65568 | tf_op jit(solution)/shard_map/ppermute | solution.py:110
  115.6 0.5 copy-done.1
  116.1 2.8 %convolution_bitcast_fusion = f32[8,128,32,32]{1,2,3,0:T(8,128)} fusion(bf16[128,32,128]{2,1,0:T(8,128)(2,1)S(1)} %dynamic-slice_bitcast_fusion, f32[128,8]{0,1:T(8,128)S(1)} %convolution_bitcast_fusion.3, bf16[128,8,64]{0,2,1:T(8,128)(2,1)S(1)} %copy-done.1, f32[64]{0:T(128)S(1)} %copy-done.8, f32[128,8]{0,1:T(8,128)S(1)} %add_rsqrt_fusion.2, ...), kind=kOutput, calls=%fused_computation.2 | convolution fusion | flops 273022976 | bytes 5390592 | tf_op jit(solution)/shard_map/while/body/eval_jaxpr/dot_general | solution.py:121
  118.9 4.7 %copy.29 = f32[8,128,32,32]{1,0,3,2:T(8,128)S(1)} copy(f32[8,128,32,32]{1,2,3,0:T(8,128)} %convolution_bitcast_fusion) | data formatting | bytes 8388608 | tf_op jit(solution)/shard_map/while/body/eval_jaxpr/transpose | solution.py:126
  123.6 1.3 fusion.92
  124.9 0.4 multiply_reduce_fusion
  125.3 0.5 fusion.41
  125.9 2.0 %convert_reduce_fusion = (f32[1024]{0:T(1024)S(1)}, bf16[1024,128]{1,0:T(8,128)(2,1)S(1)}) fusion(f32[1024,128]{1,0:T(8,128)S(1)} %get-tuple-element.19, bf16[512,128]{1,0:T(8,128)(2,1)} %param.37, f32[1024,512]{1,0:T(8,128)S(1)} %fusion.41, bf16[128,512]{1,0:T(8,128)(2,1)} %param.35, f32[128]{0:T(128)S(1)} %copy-done.9, f32[1024]{0:T(1024)S(1)} %add_rsqrt_fusion.1, ...), kind=kOutput, calls=%fused_computation.42 | convolution fusion | flops 272628736 | bytes 3158528 | tf_op jit(solution)/shard_map/dot_general | solution.py:141
  127.9 0.4 fusion.36
  128.3 0.9 convolution_bitcast_fusion.2
  129.3 0.2 fusion.93
  129.5 0.2 fusion.59
  129.7 0.2 fusion.21
  129.9 0.1 reshape.126
  130.0 2.0 %fusion.29 = bf16[8,384]{1,0:T(8,128)(2,1)} fusion(bf16[384,384]{1,0:T(8,128)(2,1)} %param.45, f32[8,384]{1,0:T(8,128)S(1)} %reshape.126, bf16[384,384]{1,0:T(8,128)(2,1)} %param.44, bf16[8,384]{1,0:T(8,128)(2,1)S(1)} %copy-done.4, f32[384]{0:T(512)S(1)} %copy-done.7, f32[8]{0:T(128)S(1)} %add_rsqrt_fusion.3, f32[8]{0:T(128)S(1)} %broadcast_multiply_fusion.3), kind=kOutput, calls=%fused_computation.32 | convolution fusion | flops 4758528 | bytes 616000 | tf_op jit(solution)/shard_map/dot_general | solution.py:187
  (92 shorter events, 0.7 us)
Async XLA Ops:
  0.6 69.7 %copy-start = (bf16[384,384]{1,0:T(8,128)(2,1)S(1)}, bf16[384,384]{1,0:T(8,128)(2,1)}, u32[]{:S(2)}) copy-start(bf16[384,384]{1,0:T(8,128)(2,1)} %param.42) | copy-start | bytes 884740
  0.6 107.9 %copy-start.10 = (s32[128]{0:T(128)S(1)}, s32[128]{0:T(128)}, u32[]{:S(2)}) copy-start(s32[128]{0:T(128)} %param.26) | copy-start | bytes 1540
  0.7 88.7 %copy-start.5 = (s32[8,128]{1,0:T(8,128)S(1)}, s32[8,128]{1,0:T(8,128)}, u32[]{:S(2)}) copy-start(s32[8,128]{1,0:T(8,128)} %param.27) | copy-start | bytes 12292
  0.7 101.4 %copy-start.14 = (s32[128]{0:T(128)S(1)}, s32[128]{0:T(128)}, u32[]{:S(2)}) copy-start(s32[128]{0:T(128)} %param.28) | copy-start | bytes 1540
  5.3 7.5 %collective-permute-start = (bf16[128,8,32]{0,2,1:T(8,128)(2,1)S(1)}, bf16[128,8,32]{0,2,1:T(8,128)(2,1)S(1)}, u32[]{:S(2)}, u32[]{:S(2)}) collective-permute-start(bf16[128,8,32]{0,2,1:T(8,128)(2,1)S(1)} %fusion.19), channel_id=1, source_target_pairs={{0,1},{1,2},{2,3},{3,4},{4,5},{5,6},{6,7},{7,8},{8,9},{9,10},{10,1... | collective-permute-start | bytes 196616 | tf_op jit(solution)/shard_map/ppermute | solution.py:110
  12.8 6.4 %collective-permute-start.1 = (bf16[128,8,32]{0,2,1:T(8,128)(2,1)S(1)}, bf16[128,8,32]{0,2,1:T(8,128)(2,1)S(1)}, u32[]{:S(2)}, u32[]{:S(2)}) collective-permute-start(bf16[128,8,32]{0,2,1:T(8,128)(2,1)S(1)} %collective-permute-done), channel_id=1, source_target_pairs={{0,1},{1,2},{2,3},{3,4},{4,5},{5,6},{6,7},{7,8},{8,9},{9,10},{10,1... | collective-permute-start | bytes 196616 | tf_op jit(solution)/shard_map/ppermute | solution.py:110
  19.2 6.4 %collective-permute-start.2 = (bf16[128,8,32]{0,2,1:T(8,128)(2,1)S(1)}, bf16[128,8,32]{0,2,1:T(8,128)(2,1)S(1)}, u32[]{:S(2)}, u32[]{:S(2)}) collective-permute-start(bf16[128,8,32]{0,2,1:T(8,128)(2,1)S(1)} %collective-permute-done.1), channel_id=1, source_target_pairs={{0,1},{1,2},{2,3},{3,4},{4,5},{5,6},{6,7},{7,8},{8,9},{9,10},{10,1... | collective-permute-start | bytes 196616 | tf_op jit(solution)/shard_map/ppermute | solution.py:110
  25.6 6.4 %collective-permute-start.3 = (bf16[128,8,32]{0,2,1:T(8,128)(2,1)S(1)}, bf16[128,8,32]{0,2,1:T(8,128)(2,1)S(1)}, u32[]{:S(2)}, u32[]{:S(2)}) collective-permute-start(bf16[128,8,32]{0,2,1:T(8,128)(2,1)S(1)} %collective-permute-done.2), channel_id=1, source_target_pairs={{0,1},{1,2},{2,3},{3,4},{4,5},{5,6},{6,7},{7,8},{8,9},{9,10},{10,1... | collective-permute-start | bytes 196616 | tf_op jit(solution)/shard_map/ppermute | solution.py:110
  32.0 6.4 %collective-permute-start.4 = (bf16[128,8,32]{0,2,1:T(8,128)(2,1)S(1)}, bf16[128,8,32]{0,2,1:T(8,128)(2,1)S(1)}, u32[]{:S(2)}, u32[]{:S(2)}) collective-permute-start(bf16[128,8,32]{0,2,1:T(8,128)(2,1)S(1)} %collective-permute-done.3), channel_id=1, source_target_pairs={{0,1},{1,2},{2,3},{3,4},{4,5},{5,6},{6,7},{7,8},{8,9},{9,10},{10,1... | collective-permute-start | bytes 196616 | tf_op jit(solution)/shard_map/ppermute | solution.py:110
  38.4 6.4 %collective-permute-start.5 = (bf16[128,8,32]{0,2,1:T(8,128)(2,1)S(1)}, bf16[128,8,32]{0,2,1:T(8,128)(2,1)S(1)}, u32[]{:S(2)}, u32[]{:S(2)}) collective-permute-start(bf16[128,8,32]{0,2,1:T(8,128)(2,1)S(1)} %collective-permute-done.4), channel_id=1, source_target_pairs={{0,1},{1,2},{2,3},{3,4},{4,5},{5,6},{6,7},{7,8},{8,9},{9,10},{10,1... | collective-permute-start | bytes 196616 | tf_op jit(solution)/shard_map/ppermute | solution.py:110
  44.8 6.4 %collective-permute-start.6 = (bf16[128,8,32]{0,2,1:T(8,128)(2,1)S(1)}, bf16[128,8,32]{0,2,1:T(8,128)(2,1)S(1)}, u32[]{:S(2)}, u32[]{:S(2)}) collective-permute-start(bf16[128,8,32]{0,2,1:T(8,128)(2,1)S(1)} %collective-permute-done.5), channel_id=1, source_target_pairs={{0,1},{1,2},{2,3},{3,4},{4,5},{5,6},{6,7},{7,8},{8,9},{9,10},{10,1... | collective-permute-start | bytes 196616 | tf_op jit(solution)/shard_map/ppermute | solution.py:110
  51.1 19.0 %collective-permute-start.7 = (bf16[128,8,32]{0,2,1:T(8,128)(2,1)S(1)}, bf16[128,8,32]{0,2,1:T(8,128)(2,1)S(1)}, u32[]{:S(2)}, u32[]{:S(2)}) collective-permute-start(bf16[128,8,32]{0,2,1:T(8,128)(2,1)S(1)} %collective-permute-done.6), channel_id=1, source_target_pairs={{0,1},{1,2},{2,3},{3,4},{4,5},{5,6},{6,7},{7,8},{8,9},{9,10},{10,1... | collective-permute-start | bytes 196616 | tf_op jit(solution)/shard_map/ppermute | solution.py:110
  70.2 6.4 %collective-permute-start.8 = (bf16[128,8,32]{0,2,1:T(8,128)(2,1)S(1)}, bf16[128,8,32]{0,2,1:T(8,128)(2,1)S(1)}, u32[]{:S(2)}, u32[]{:S(2)}) collective-permute-start(bf16[128,8,32]{0,2,1:T(8,128)(2,1)S(1)} %collective-permute-done.7), channel_id=1, source_target_pairs={{0,1},{1,2},{2,3},{3,4},{4,5},{5,6},{6,7},{7,8},{8,9},{9,10},{10,1... | collective-permute-start | bytes 196616 | tf_op jit(solution)/shard_map/ppermute | solution.py:110
  76.5 6.4 %collective-permute-start.9 = (bf16[128,8,32]{0,2,1:T(8,128)(2,1)S(1)}, bf16[128,8,32]{0,2,1:T(8,128)(2,1)S(1)}, u32[]{:S(2)}, u32[]{:S(2)}) collective-permute-start(bf16[128,8,32]{0,2,1:T(8,128)(2,1)S(1)} %collective-permute-done.8), channel_id=1, source_target_pairs={{0,1},{1,2},{2,3},{3,4},{4,5},{5,6},{6,7},{7,8},{8,9},{9,10},{10,1... | collective-permute-start | bytes 196616 | tf_op jit(solution)/shard_map/ppermute | solution.py:110
  82.9 6.4 %collective-permute-start.10 = (bf16[128,8,32]{0,2,1:T(8,128)(2,1)S(1)}, bf16[128,8,32]{0,2,1:T(8,128)(2,1)S(1)}, u32[]{:S(2)}, u32[]{:S(2)}) collective-permute-start(bf16[128,8,32]{0,2,1:T(8,128)(2,1)S(1)} %collective-permute-done.9), channel_id=1, source_target_pairs={{0,1},{1,2},{2,3},{3,4},{4,5},{5,6},{6,7},{7,8},{8,9},{9,10},{10,1... | collective-permute-start | bytes 196616 | tf_op jit(solution)/shard_map/ppermute | solution.py:110
  89.3 6.4 %collective-permute-start.11 = (bf16[128,8,32]{0,2,1:T(8,128)(2,1)S(1)}, bf16[128,8,32]{0,2,1:T(8,128)(2,1)S(1)}, u32[]{:S(2)}, u32[]{:S(2)}) collective-permute-start(bf16[128,8,32]{0,2,1:T(8,128)(2,1)S(1)} %collective-permute-done.10), channel_id=1, source_target_pairs={{0,1},{1,2},{2,3},{3,4},{4,5},{5,6},{6,7},{7,8},{8,9},{9,10},{10,1... | collective-permute-start | bytes 196616 | tf_op jit(solution)/shard_map/ppermute | solution.py:110
  95.7 6.4 %collective-permute-start.12 = (bf16[128,8,32]{0,2,1:T(8,128)(2,1)S(1)}, bf16[128,8,32]{0,2,1:T(8,128)(2,1)S(1)}, u32[]{:S(2)}, u32[]{:S(2)}) collective-permute-start(bf16[128,8,32]{0,2,1:T(8,128)(2,1)S(1)} %collective-permute-done.11), channel_id=1, source_target_pairs={{0,1},{1,2},{2,3},{3,4},{4,5},{5,6},{6,7},{7,8},{8,9},{9,10},{10,1... | collective-permute-start | bytes 196616 | tf_op jit(solution)/shard_map/ppermute | solution.py:110
  102.1 6.4 %collective-permute-start.13 = (bf16[128,8,32]{0,2,1:T(8,128)(2,1)S(1)}, bf16[128,8,32]{0,2,1:T(8,128)(2,1)S(1)}, u32[]{:S(2)}, u32[]{:S(2)}) collective-permute-start(bf16[128,8,32]{0,2,1:T(8,128)(2,1)S(1)} %collective-permute-done.12), channel_id=1, source_target_pairs={{0,1},{1,2},{2,3},{3,4},{4,5},{5,6},{6,7},{7,8},{8,9},{9,10},{10,1... | collective-permute-start | bytes 196616 | tf_op jit(solution)/shard_map/ppermute | solution.py:110
  108.5 6.4 %collective-permute-start.14 = (bf16[128,8,32]{0,2,1:T(8,128)(2,1)S(1)}, bf16[128,8,32]{0,2,1:T(8,128)(2,1)S(1)}, u32[]{:S(2)}, u32[]{:S(2)}) collective-permute-start(bf16[128,8,32]{0,2,1:T(8,128)(2,1)S(1)} %collective-permute-done.13), channel_id=1, source_target_pairs={{0,1},{1,2},{2,3},{3,4},{4,5},{5,6},{6,7},{7,8},{8,9},{9,10},{10,1... | collective-permute-start | bytes 196616 | tf_op jit(solution)/shard_map/ppermute | solution.py:110
  115.2 0.9 copy-start.1
  115.2 0.9 copy-start.6
  115.2 0.9 copy-start.8
  118.9 4.7 %copy-start.11 = (bf16[1024,128]{1,0:T(8,128)(2,1)S(1)}, bf16[1024,128]{1,0:T(8,128)(2,1)}, u32[]{:S(2)}) copy-start(bf16[1024,128]{1,0:T(8,128)(2,1)} %param.32) | copy-start | bytes 786436
  118.9 4.7 %copy-start.12 = (bf16[8,128,128]{2,1,0:T(8,128)(2,1)S(1)}, bf16[8,128,128]{2,1,0:T(8,128)(2,1)}, u32[]{:S(2)}) copy-start(bf16[8,128,128]{2,1,0:T(8,128)(2,1)} %param.24) | copy-start | bytes 786436
  118.9 4.7 %copy-start.15 = (f32[128]{0:T(128)S(1)}, f32[128]{0:T(128)}, u32[]{:S(2)}) copy-start(f32[128]{0:T(128)} %param.33) | copy-start | bytes 1540
  123.6 1.7 %copy-start.3 = (bf16[128,512]{1,0:T(8,128)(2,1)S(1)}, bf16[128,512]{1,0:T(8,128)(2,1)}, u32[]{:S(2)}) copy-start(bf16[128,512]{1,0:T(8,128)(2,1)} %param.36) | copy-start | bytes 393220
  123.6 1.7 %copy-start.9 = (f32[128]{0:T(128)S(1)}, f32[128]{0:T(128)}, u32[]{:S(2)}) copy-start(f32[128]{0:T(128)} %param.34) | copy-start | bytes 1540
  125.8 2.5 %copy-start.13 = (bf16[128,16]{0,1:T(8,128)(2,1)S(1)}, bf16[128,16]{0,1:T(8,128)(2,1)}, u32[]{:S(2)}) copy-start(bf16[128,16]{0,1:T(8,128)(2,1)} %param.39) | copy-start | bytes 12292
  125.8 2.5 %copy-start.16 = (f32[128]{0:T(128)S(1)}, f32[128]{0:T(128)}, u32[]{:S(2)}) copy-start(f32[128]{0:T(128)} %param.38) | copy-start | bytes 1540
  125.8 4.2 %copy-start.4 = (bf16[8,384]{1,0:T(8,128)(2,1)S(1)}, bf16[8,384]{1,0:T(8,128)(2,1)}, u32[]{:S(2)}) copy-start(bf16[8,384]{1,0:T(8,128)(2,1)} %param.25) | copy-start | bytes 18436
  125.8 4.2 %copy-start.7 = (f32[384]{0:T(512)S(1)}, f32[384]{0:T(512)}, u32[]{:S(2)}) copy-start(f32[384]{0:T(512)} %param.40) | copy-start | bytes 4612
  127.9 4.1 %copy-start.2 = (bf16[1024,128]{1,0:T(8,128)(2,1)}, bf16[1024,128]{1,0:T(8,128)(2,1)S(1)}, u32[]{:S(2)}) copy-start(bf16[1024,128]{1,0:T(8,128)(2,1)S(1)} %get-tuple-element.21) | copy-start | bytes 786436
